TPU v7x, 32 devices: a whole 2x2x4 slice. The times are simulated.
32 devices in a mesh: cache: 8 (over z, x), expert: 4 (over y, core).
Axes of the slice: x: 2, y: 2, z: 4, core: 2. Of those that a mesh axis runs over, the one named last changes fastest.
Arguments:
- query: bfloat16 [512, 2048], P('cache', 'expert'), may hold values from -8 to 8
- new_key: bfloat16 [512, 512], P('cache', 'expert'), may hold values from -8 to 8
- new_value: bfloat16 [512, 512], P('cache', 'expert'), may hold values from -6 to 6
- private_keys: bfloat16 [512, 64, 512], P('cache', None, 'expert'), may hold values from -8 to 8
- private_values: bfloat16 [512, 64, 512], P('cache', None, 'expert'), may hold values from -6 to 6
- private_lengths: int32 [512], P('cache'), may hold values from 1 to 64
- prefix_keys: bfloat16 [16, 1024, 512], P('cache', None, 'expert'), may hold values from -8 to 8
- prefix_values: bfloat16 [16, 1024, 512], P('cache', None, 'expert'), may hold values from -6 to 6
- slot_group: int32 [16], replicated, may hold values from 0 to 15, each once
- group_ids: int32 [512, 1], P('cache'), may hold values from 0 to 15; in each aligned block of 64 rows (0 to 63, 64 to 127, ...) at most 8 rows name the same one
- out_weight: bfloat16 [2048, 4096], P('expert', 'cache'), may hold values from -0.125 to 0.125
- hidden_in: bfloat16 [512, 4096], P(('cache', 'expert')), may hold values from -6 to 6
- norm_gain: float32 [4096], replicated, may hold values from 0.1 to 1.9
- expert_ids: int32 [512, 2], P(('cache', 'expert')), may hold values from 0 to 3, all different within a row; in each aligned block of 16 rows (0 to 15, 16 to 31, ...) at most 16 rows name the same one
- gate_weights: float32 [512, 2], P(('cache', 'expert')), may hold values from 0.1 to 0.9
- w_gate: bfloat16 [4, 4096, 14336], P('expert', None, 'cache'), may hold values from -0.09375 to 0.09375
- w_up: bfloat16 [4, 4096, 14336], P('expert', None, 'cache'), may hold values from -0.09375 to 0.09375
- w_down: bfloat16 [4, 14336, 4096], P('expert', 'cache'), may hold values from -0.046875 to 0.046875
Outputs:
- attention: bfloat16 [512, 2048], P('cache', 'expert')
- layer_out: bfloat16 [512, 4096], P(('cache', 'expert'))
Inputs may be any that keep to these rules, and one draw needn't show every extreme that they name: `group_ids`: within each aligned block of 64 requests at most 8 name one group. `slot_group`: each group is held by exactly one slot. `private_lengths`: positions 0 to length - 1 of a request's private cache are live. `expert_ids`: each token names two different experts; among the 16 tokens of one device at most 16 name one expert.
All inputs are finite; a program needn't handle non-finite values.
Results may differ from a plain program's by a relative error of at most 0.0095.
Values may be sent and summed in bfloat16 or wider, within the bound.
A program may use at most 128 MiB of HBM per device.

v0:
```python
import math
import jax
import jax.numpy as jnp
from jax import lax
from jax.sharding import PartitionSpec as P

MOSTG = 8
NEG = -1e30
EPSILON = 1e-05


def private_partial(queries, keys, values, lengths, new_key, new_value, scale):
    scores = jnp.einsum("rhd,rpd->rhp", queries, keys, preferred_element_type=jnp.float32) * scale
    live = jnp.arange(keys.shape[1], dtype=jnp.int32)[None, :] < lengths[:, None]
    scores = jnp.where(live[:, None, :], scores, NEG)
    fresh = jnp.einsum("rhd,rd->rh", queries, new_key, preferred_element_type=jnp.float32) * scale
    top = jnp.maximum(jnp.max(scores, axis=-1), fresh)
    expo = jnp.where(live[:, None, :], jnp.exp(scores - top[..., None]), 0.0)
    fresh_expo = jnp.exp(fresh - top)
    total = jnp.sum(expo, axis=-1) + fresh_expo
    summed = jnp.einsum(
        "rhp,rpd->rhd", expo.astype(jnp.bfloat16), values, preferred_element_type=jnp.float32
    )
    fresh_weight = lax.optimization_barrier(fresh_expo.astype(jnp.bfloat16)).astype(jnp.float32)
    summed = summed + fresh_weight[..., None] * new_value.astype(jnp.float32)[:, None, :]
    return (summed / total[..., None], top + jnp.log(total))


def prefix_partial(received, prefix_keys, prefix_values, scale):
    rows, heads, width = received.shape
    slots = prefix_keys.shape[0]
    blocks = received.reshape(rows // (slots * MOSTG), slots, MOSTG, heads, width)
    scores = (
        jnp.einsum("cgmhd,gpd->cgmhp", blocks, prefix_keys, preferred_element_type=jnp.float32)
        * scale
    )
    top = jnp.max(scores, axis=-1)
    expo = jnp.exp(scores - top[..., None])
    total = jnp.sum(expo, axis=-1)
    summed = jnp.einsum(
        "cgmhp,gpd->cgmhd",
        expo.astype(jnp.bfloat16),
        prefix_values,
        preferred_element_type=jnp.float32,
    )
    outputs = (summed / total[..., None]).reshape(rows, heads, width)
    return (outputs, (top + jnp.log(total)).reshape(rows, heads))


def on_device(
    query,
    new_key,
    new_value,
    private_keys,
    private_values,
    private_lengths,
    prefix_keys,
    prefix_values,
    slot_group,
    group_ids,
    out_weight,
    hidden_in,
    norm_gain,
    expert_ids,
    gate_weights,
    w_gate,
    w_up,
    w_down,
):
    head_dim = new_key.shape[1]
    requests = query.shape[0]
    heads = query.shape[1] // head_dim
    scale = 1.0 / math.sqrt(head_dim)
    queries = query.reshape(requests, heads, head_dim)
    near_out, near_lse = private_partial(
        queries, private_keys, private_values, private_lengths, new_key, new_value, scale
    )
    slot_count = slot_group.shape[0]
    matches = group_ids[:, 0][:, None] == slot_group[None, :]
    slot = jnp.sum(jnp.where(matches, jnp.arange(slot_count, dtype=jnp.int32)[None, :], 0), axis=1)
    order = jnp.arange(requests, dtype=jnp.int32)
    earlier = order[None, :] < order[:, None]
    rank = jnp.sum((slot[:, None] == slot[None, :]) & earlier, axis=1)
    position = slot * MOSTG + rank
    places = jnp.arange(slot_count * MOSTG, dtype=jnp.int32)
    placing = places[:, None] == position[None, :]
    sent = jnp.dot(placing.astype(jnp.bfloat16), query, preferred_element_type=jnp.float32).astype(
        jnp.bfloat16
    )
    sent = sent.reshape(slot_count * MOSTG, heads, head_dim)
    outputs, lse_part = prefix_partial(
        lax.all_to_all(sent, "cache", split_axis=0, concat_axis=0, tiled=True),
        prefix_keys,
        prefix_values,
        scale,
    )
    back_out = lax.all_to_all(outputs, "cache", split_axis=0, concat_axis=0, tiled=True)
    back_lse = lax.all_to_all(lse_part, "cache", split_axis=0, concat_axis=0, tiled=True)
    taking = placing.astype(jnp.float32)
    far_out = jnp.einsum("sr,shd->rhd", taking, back_out, precision=lax.Precision.HIGHEST)
    far_lse = jnp.einsum("sr,sh->rh", taking, back_lse, precision=lax.Precision.HIGHEST)
    both = jnp.logaddexp(near_lse, far_lse)
    merged = (
        near_out * jnp.exp(near_lse - both)[..., None]
        + far_out * jnp.exp(far_lse - both)[..., None]
    )
    attention = merged.astype(jnp.bfloat16).reshape(requests, heads * head_dim)
    experts = lax.axis_size("expert")
    tokens = hidden_in.shape[0]
    terms = jnp.dot(
        lax.all_gather(attention, "cache", axis=0, tiled=True),
        out_weight,
        preferred_element_type=jnp.float32,
    )
    regrouped = lax.all_to_all(
        terms.astype(jnp.bfloat16), "cache", split_axis=0, concat_axis=1, tiled=True
    ).astype(terms.dtype)
    proj = lax.psum_scatter(
        regrouped.astype(jnp.bfloat16), "expert", scatter_dimension=0, tiled=True
    ).astype(jnp.float32)
    resid = hidden_in.astype(jnp.float32) + proj
    normed = (
        resid * lax.rsqrt(jnp.mean(resid * resid, axis=-1, keepdims=True) + EPSILON) * norm_gain
    ).astype(jnp.bfloat16)
    capacity = max(2, 4 * tokens // experts)
    flat_ids = expert_ids.reshape(-1)
    order_ids = jnp.arange(flat_ids.shape[0], dtype=jnp.int32)
    before = order_ids[None, :] < order_ids[:, None]
    slot_rank = jnp.sum((flat_ids[:, None] == flat_ids[None, :]) & before, axis=1)
    destination = flat_ids * capacity + slot_rank
    expert_slots = jnp.arange(experts * capacity, dtype=jnp.int32)
    chosen = (destination[None, :] == expert_slots[:, None]).reshape(experts * capacity, tokens, 2)
    picking = jnp.sum(chosen.astype(jnp.bfloat16), axis=2)
    outgoing = jnp.dot(picking, normed, preferred_element_type=jnp.float32).astype(jnp.bfloat16)
    arrived = lax.all_to_all(outgoing, "expert", split_axis=0, concat_axis=0, tiled=True)
    piece = lax.all_gather(arrived, "cache", axis=0, tiled=True)
    gate = jnp.dot(piece, w_gate[0], preferred_element_type=jnp.float32)
    up = jnp.dot(piece, w_up[0], preferred_element_type=jnp.float32)
    act = (jax.nn.silu(gate) * up).astype(jnp.bfloat16)
    partial_out = jnp.dot(act, w_down[0], preferred_element_type=jnp.float32)
    summed_rows = lax.psum_scatter(
        partial_out.astype(jnp.bfloat16), "cache", scatter_dimension=0, tiled=True
    )
    returned = lax.all_to_all(summed_rows, "expert", split_axis=0, concat_axis=0, tiled=True)
    mixing = jnp.sum(jnp.where(chosen, gate_weights[None, :, :], 0.0), axis=2)
    moe = jnp.einsum(
        "st,sd->td", mixing, returned.astype(jnp.float32), precision=lax.Precision.HIGHEST
    )
    layer_out = (resid + moe).astype(jnp.bfloat16)
    return (attention, layer_out)


def solution(mesh):
    in_specs = (
        P("cache", "expert"),
        P("cache", "expert"),
        P("cache", "expert"),
        P("cache", None, "expert"),
        P("cache", None, "expert"),
        P("cache"),
        P("cache", None, "expert"),
        P("cache", None, "expert"),
        P(),
        P("cache", None),
        P("expert", "cache"),
        P(("cache", "expert"), None),
        P(),
        P(("cache", "expert"), None),
        P(("cache", "expert"), None),
        P("expert", None, "cache"),
        P("expert", None, "cache"),
        P("expert", "cache", None),
    )
    out_specs = (P("cache", "expert"), P(("cache", "expert"), None))
    return jax.shard_map(
        on_device, mesh=mesh, in_specs=in_specs, out_specs=out_specs, check_vma=False
    )
```

profile of v0, /device:TPU:0, one launch (start us, length us, event | category | flops | bytes accessed | tf_op | source)
XLA Modules:
  0.0 354.4 jit_solution(17689900936632118236)
XLA Ops:
  7.2 0.8 select_reduce_fusion.1
  8.0 0.2 convert_reduce_fusion
  8.2 1.1 convolution_convert_fusion.2
  9.4 0.7 reshape.100
  10.1 7.3 %all-to-all-start = ((bf16[128,4,128]{2,1,0:T(4,128)(2,1)}), bf16[128,4,128]{2,1,0:T(4,128)(2,1)S(1)}, u32[]{:S(2)}, u32[]{:S(2)}) async-start(bf16[128,4,128]{2,1,0:T(4,128)(2,1)} %reshape.100), calls=%async_computation | async-start | bytes 262144 | tf_op jit(solution)/shard_map/all_to_all | solution.py:92
  17.3 0.9 reshape.99
  18.2 0.7 iota_compare_fusion.4
  18.9 2.0 fusion.61
  20.9 0.9 fusion.45
  22.0 0.1 copy.110
  22.1 2.6 all-to-all-done
  24.7 1.6 bitcast_reduce_fusion
  26.3 0.5 fusion.17
  26.8 0.7 reshape.109
  27.5 3.4 all-to-all-start.1
  31.0 1.6 fusion.18
  32.6 0.9 copy.121
  33.5 4.1 %all-to-all-done.1 = f32[8,16,4]{1,2,0:T(4,128)S(1)} async-done(((f32[8,16,4]{1,2,0:T(4,128)}), f32[8,16,4]{1,2,0:T(4,128)S(1)}, u32[]{:S(2)}, u32[]{:S(2)}) %all-to-all-start.1) | async-done | bytes 2080 | tf_op jit(solution)/shard_map/all_to_all | solution.py:98
  37.5 3.4 all-to-all-start.2
  41.0 0.2 fusion.35
  41.3 0.1 copy.111
  41.5 0.2 subtract_exponential_fusion.1
  41.8 0.1 copy.113
  41.9 0.1 copy.123
  42.0 0.1 copy.119
  42.1 7.0 %all-to-all-done.2 = f32[128,4,128]{2,1,0:T(4,128)S(1)} async-done(((f32[128,4,128]{2,1,0:T(4,128)}), f32[128,4,128]{2,1,0:T(4,128)S(1)}, u32[]{:S(2)}, u32[]{:S(2)}) %all-to-all-start.2) | async-done | bytes 262176 | tf_op jit(solution)/shard_map/all_to_all | solution.py:97
  49.1 0.2 fusion.30
  49.4 0.5 fusion.23
  49.9 31.7 %all_gather.6 = bf16[512,512]{1,0:T(8,128)(2,1)S(1)} all-gather(bf16[64,512]{1,0:T(8,128)(2,1)S(1)} %bitcast.102), channel_id=1, replica_groups=mesh['cache'=8,'expert'=4] {'cache'}, dimensions={0}, use_global_device_ids=true | all-gather | bytes 589824 | tf_op jit(solution)/shard_map/all_gather | solution.py:111
  81.6 0.4 convolution_convert_fusion.1
  82.0 13.0 %all_to_all.62 = bf16[8,64,512]{2,1,0:T(8,128)(2,1)S(1)} all-to-all(bf16[8,64,512]{2,1,0:T(8,128)(2,1)S(1)} %bitcast.92), channel_id=1, replica_groups=mesh['cache'=8,'expert'=4] {'cache'}, dimensions={0} | all-to-all | bytes 1048576 | tf_op jit(solution)/shard_map/all_to_all | solution.py:115
  95.1 0.8 copy.136
  96.0 0.1 copy.126
  96.1 0.1 eq.80
  96.2 0.2 convert_reduce_fusion.1
  96.4 0.1 copy.127
  96.6 20.2 %reduce-scatter.3.cloned.1.call-done = bf16[16,4096]{1,0:T(8,128)(2,1)} async-done(((bf16[64,4096]{1,0:T(8,128)(2,1)}), bf16[16,4096]{1,0:T(8,128)(2,1)}) %reduce-scatter.3.cloned.1.call-update) | async-done | bytes 131088 | tf_op jit(solution)/shard_map/reduce_scatter | solution.py:118
  116.8 1.1 multiply_reduce_fusion
  117.9 1.2 convolution_convert_fusion
  119.1 11.9 %all_to_all.63 = bf16[4,16,4096]{2,1,0:T(8,128)(2,1)} all-to-all(bf16[4,16,4096]{2,1,0:T(8,128)(2,1)S(1)} %bitcast.96), channel_id=1, replica_groups=mesh['cache'=8,'expert'=4] {'expert'}, dimensions={0} | all-to-all | bytes 1048576 | tf_op jit(solution)/shard_map/all_to_all | solution.py:135
  131.0 0.2 reduce-scatter.5.cloned.1.call-start
  131.3 72.7 %all-gather.2.cloned.1.call-done = bf16[512,4096]{1,0:T(8,128)(2,1)} async-done(((bf16[64,4096]{1,0:T(8,128)(2,1)}), bf16[512,4096]{1,0:T(8,128)(2,1)}) %all-gather.2.cloned.1.call-update) | async-done | bytes 4194320 | tf_op jit(solution)/shard_map/all_gather | solution.py:136
  204.0 14.6 %fusion.4 = f32[512,1792]{1,0:T(8,128)} fusion(bf16[512,4096]{1,0:T(8,128)(2,1)} %all-gather.2.cloned.1.call-done, bf16[1,4096,1792]{2,1,0:T(8,128)(2,1)} %param.33), kind=kOutput, calls=%fused_computation.4 | convolution fusion | flops 7516192768 | bytes 22544384 | tf_op jit(solution)/shard_map/dot_general | solution.py:137
  218.6 28.7 %fusion.6 = bf16[512,4096]{1,0:T(8,128)(2,1)} fusion(bf16[1,1792,4096]{2,1,0:T(8,128)(2,1)} %param.35, f32[512,1792]{1,0:T(8,128)} %fusion.4, bf16[512,4096]{1,0:T(8,128)(2,1)} %all-gather.2.cloned.1.call-done, bf16[1,4096,1792]{2,1,0:T(8,128)(2,1)} %param.34), kind=kOutput, calls=%fused_computation.6 | convolution fusion | flops 15039987712 | bytes 41418752 | tf_op jit(solution)/shard_map/dot_general | solution.py:140
  247.3 87.4 %reduce-scatter.5.cloned.1.call-done = bf16[64,4096]{1,0:T(8,128)(2,1)} async-done(((bf16[512,4096]{1,0:T(8,128)(2,1)}), bf16[64,4096]{1,0:T(8,128)(2,1)}) %reduce-scatter.5.cloned.1.call-update) | async-done | bytes 524304 | tf_op jit(solution)/shard_map/reduce_scatter | solution.py:141
  334.6 3.5 all-to-all-start.5
  338.2 8.7 %all-to-all-done.5 = bf16[4,16,4096]{2,1,0:T(8,128)(2,1)S(1)} async-done(((bf16[4,16,4096]{2,1,0:T(8,128)(2,1)}), bf16[4,16,4096]{2,1,0:T(8,128)(2,1)S(1)}, u32[]{:S(2)}, u32[]{:S(2)}) %all-to-all-start.5) | async-done | bytes 524320 | tf_op jit(solution)/shard_map/all_to_all | solution.py:144
  346.9 1.0 fusion.9
  (43 shorter events, 0.9 us)
Async XLA Ops:
  7.2 42.2 %copy-start = (bf16[64,64,128]{2,1,0:T(8,128)(2,1)S(1)}, bf16[64,64,128]{2,1,0:T(8,128)(2,1)}, u32[]{:S(2)}) copy-start(bf16[64,64,128]{2,1,0:T(8,128)(2,1)} %param.22) | copy-start | bytes 3145732
  10.1 14.6 %all-to-all-start = ((bf16[128,4,128]{2,1,0:T(4,128)(2,1)}), bf16[128,4,128]{2,1,0:T(4,128)(2,1)S(1)}, u32[]{:S(2)}, u32[]{:S(2)}) async-start(bf16[128,4,128]{2,1,0:T(4,128)(2,1)} %reshape.100), calls=%async_computation | async-start | bytes 262144 | tf_op jit(solution)/shard_map/all_to_all | solution.py:92
  26.3 15.2 %copy-start.6 = (bf16[64,128]{1,0:T(8,128)(2,1)S(1)}, bf16[64,128]{1,0:T(8,128)(2,1)}, u32[]{:S(2)}) copy-start(bf16[64,128]{1,0:T(8,128)(2,1)} %param.20) | copy-start | bytes 49156
  27.5 10.0 %all-to-all-start.1 = ((f32[8,16,4]{1,2,0:T(4,128)}), f32[8,16,4]{1,2,0:T(4,128)S(1)}, u32[]{:S(2)}, u32[]{:S(2)}) async-start(f32[8,16,4]{1,2,0:T(4,128)} %reshape.109), calls=%async_computation.1 | async-start | bytes 32768 | tf_op jit(solution)/shard_map/all_to_all | solution.py:98
  32.6 49.0 %copy-start.4 = (bf16[512,512]{1,0:T(8,128)(2,1)S(1)}, bf16[512,512]{1,0:T(8,128)(2,1)}, u32[]{:S(2)}) copy-start(bf16[512,512]{1,0:T(8,128)(2,1)} %param.28) | copy-start | bytes 1572868
  37.5 11.6 %all-to-all-start.2 = ((f32[128,4,128]{2,1,0:T(4,128)}), f32[128,4,128]{2,1,0:T(4,128)S(1)}, u32[]{:S(2)}, u32[]{:S(2)}) async-start(f32[128,4,128]{2,1,0:T(4,128)} %copy.121), calls=%async_computation.2 | async-start | bytes 524288 | tf_op jit(solution)/shard_map/all_to_all | solution.py:97
  41.0 75.8 %reduce-scatter.3.cloned.1.call-start = ((), (), s32[]{:S(2)}) async-start(), calls=%async_computation.8 | async-start | bytes 655360 | tf_op jit(solution)/shard_map/reduce_scatter | solution.py:118
  49.4 46.6 %copy-start.8 = (s32[16,2]{0,1:T(2,128)S(1)}, s32[16,2]{0,1:T(2,128)}, u32[]{:S(2)}) copy-start(s32[16,2]{0,1:T(2,128)} %param.31) | copy-start | bytes 388
  49.4 67.4 %copy-start.2 = (bf16[16,4096]{1,0:T(8,128)(2,1)S(1)}, bf16[16,4096]{1,0:T(8,128)(2,1)}, u32[]{:S(2)}) copy-start(bf16[16,4096]{1,0:T(8,128)(2,1)} %param.29) | copy-start | bytes 393220
  49.4 68.4 %copy-start.7 = (f32[4096]{0:T(1024)S(1)}, f32[4096]{0:T(1024)}, u32[]{:S(2)}) copy-start(f32[4096]{0:T(1024)} %param.30) | copy-start | bytes 49156
  49.9 81.1 %copy-start.5 = (bf16[8,8,4,128]{3,1,2,0:T(8,128)(2,1)}, bf16[8,8,4,128]{3,1,2,0:T(8,128)(2,1)S(1)}, u32[]{:S(2)}) copy-start(bf16[8,8,4,128]{3,1,2,0:T(8,128)(2,1)S(1)} %copy.150) | copy-start | bytes 196612
  95.9 108.0 %all-gather.2.cloned.1.call-start = ((), (), s32[]{:S(2)}) async-start(), calls=%async_computation.9 | async-start | bytes 4718592 | tf_op jit(solution)/shard_map/all_gather | solution.py:136
  131.0 203.6 %reduce-scatter.5.cloned.1.call-start = ((), (), s32[]{:S(2)}) async-start(), calls=%async_computation.10 | async-start | bytes 4718592 | tf_op jit(solution)/shard_map/reduce_scatter | solution.py:141
  218.6 129.3 %copy-start.1 = (bf16[64,64,128]{2,1,0:T(8,128)(2,1)S(1)}, bf16[64,64,128]{2,1,0:T(8,128)(2,1)}, u32[]{:S(2)}) copy-start(bf16[64,64,128]{2,1,0:T(8,128)(2,1)} %param.22) | copy-start | bytes 3145732
  247.2 90.9 %copy-start.9 = (f32[16,2]{0,1:T(2,128)S(1)}, f32[16,2]{0,1:T(2,128)}, u32[]{:S(2)}) copy-start(f32[16,2]{0,1:T(2,128)} %param.32) | copy-start | bytes 388
  247.2 99.7 %copy-start.3 = (bf16[16,4096]{1,0:T(8,128)(2,1)S(1)}, bf16[16,4096]{1,0:T(8,128)(2,1)}, u32[]{:S(2)}) copy-start(bf16[16,4096]{1,0:T(8,128)(2,1)} %reduce-scatter.3.cloned.1.call-done) | copy-start | bytes 393220
  334.6 12.3 %all-to-all-start.5 = ((bf16[4,16,4096]{2,1,0:T(8,128)(2,1)}), bf16[4,16,4096]{2,1,0:T(8,128)(2,1)S(1)}, u32[]{:S(2)}, u32[]{:S(2)}) async-start(bf16[4,16,4096]{2,1,0:T(8,128)(2,1)} %bitcast.100), calls=%async_computation.7 | async-start | bytes 1048576 | tf_op jit(solution)/shard_map/all_to_all | solution.py:144
Sparse Core Ops, SparseCore 0:
  96.0 20.6 reduce-scatter.2
  131.2 72.7 all-gather.1
  247.4 87.2 reduce-scatter.4
where the time goes:
time: 355 us; the launch traced here: 354 us
  waiting for transfers between devices  203 us (57%)
  blocking collectives  56.6 us (16%)
  matrix products  54 us (15%)
  starting transfers between devices  17.9 us (5%)
  between operations  14 us (4%)
  local copies, waits for them, and re-layouts  5.2 us (1%)
  other arithmetic  3.97 us (1%)
    reduce_scatter x1, waiting for transfers between devices, on_device(): lax.psum_scatter(partial_out.astype(jnp.bfloat16), 'cache', scatter_dimen...  87.4 us
    all_gather x1, waiting for transfers between devices, on_device(): piece = lax.all_gather(arrived, 'cache', axis=0, tiled=True)  72.7 us
    all_gather x1, blocking collectives, on_device(): lax.all_gather(attention, 'cache', axis=0, tiled=True)  31.7 us
    dot_general x1, matrix products, on_device(): partial_out = jnp.dot(act, w_down[0], preferred_element_type=jnp.float32)  28.7 us
    reduce_scatter x1, waiting for transfers between devices, on_device(): lax.psum_scatter(regrouped.astype(jnp.bfloat16), 'expert', scatter_dimens...  20.2 us
    dot_general x1, matrix products, on_device(): gate = jnp.dot(piece, w_gate[0], preferred_element_type=jnp.float32)  14.6 us
    all_to_all x1, blocking collectives, on_device(): lax.all_to_all(terms.astype(jnp.bfloat16), 'cache', split_axis=0, concat_...  13 us
    all_to_all x1, blocking collectives, on_device(): lax.all_to_all(outgoing, 'expert', split_axis=0, concat_axis=0, tiled=True)  11.9 us
  transfers between devices with their start and end apart: 7, of which 7 were waited for; matrix products, arithmetic and copies ran while one was open for 2% of the time, Pallas kernels for 0%

commit v1 on v0

--- a/solution.py
+++ b/solution.py
@@ -133,7 +133,10 @@
     picking = jnp.sum(chosen.astype(jnp.bfloat16), axis=2)
     outgoing = jnp.dot(picking, normed, preferred_element_type=jnp.float32).astype(jnp.bfloat16)
     arrived = lax.all_to_all(outgoing, "expert", split_axis=0, concat_axis=0, tiled=True)
-    piece = lax.all_gather(arrived, "cache", axis=0, tiled=True)
+    n_dev = lax.axis_size("cache")
+    pieces = jnp.stack([arrived for _ in range(n_dev)])
+    pieces = lax.all_to_all(pieces, "cache", split_axis=0, concat_axis=0)
+    piece = jnp.concatenate(pieces, axis=0)
     gate = jnp.dot(piece, w_gate[0], preferred_element_type=jnp.float32)
     up = jnp.dot(piece, w_up[0], preferred_element_type=jnp.float32)
     act = (jax.nn.silu(gate) * up).astype(jnp.bfloat16)

time: 355 us -> 380 us (1.070)
  blocking collectives: 56.6 us -> 154 us
  waiting for transfers between devices: 203 us -> 129 us
    all_to_all x0 -> x1, blocking collectives: none -> 98.4 us  [on_device(): pieces = lax.all_to_all(pieces, 'cache', split_axis=0, concat_axis=0)]
    all_gather x1 -> x0, waiting for transfers between devices: 72.7 us -> none  [on_device(): piece = lax.all_gather(arrived, 'cache', axis=0, tiled=True)]
  transfers between devices with their start and end apart: 7 -> 6, of which waited for: 7 -> 6; matrix products, arithmetic and copies ran while one was open for 2% -> 2% of each run, Pallas kernels for 0% -> 0%
where the time goes in v1:
time: 380 us; the launch traced here: 379 us
  blocking collectives  154 us (41%)
  waiting for transfers between devices  129 us (34%)
  matrix products  52.3 us (14%)
  starting transfers between devices  17.7 us (5%)
  between operations  14.3 us (4%)
  local copies, waits for them, and re-layouts  7.69 us (2%)
  other arithmetic  3.97 us (1%)
    all_to_all x1, blocking collectives, on_device(): pieces = lax.all_to_all(pieces, 'cache', split_axis=0, concat_axis=0)  98.4 us
    reduce_scatter x1, waiting for transfers between devices, on_device(): lax.psum_scatter(partial_out.astype(jnp.bfloat16), 'cache', scatter_dimen...  86.6 us
    all_gather x1, blocking collectives, on_device(): lax.all_gather(attention, 'cache', axis=0, tiled=True)  31.7 us
    dot_general x1, matrix products, on_device(): partial_out = jnp.dot(act, w_down[0], preferred_element_type=jnp.float32)  28.6 us
    reduce_scatter x1, waiting for transfers between devices, on_device(): lax.psum_scatter(regrouped.astype(jnp.bfloat16), 'expert', scatter_dimens...  20.2 us
    all_to_all x1, blocking collectives, on_device(): lax.all_to_all(terms.astype(jnp.bfloat16), 'cache', split_axis=0, concat_...  13 us
    dot_general x1, matrix products, on_device(): gate = jnp.dot(piece, w_gate[0], preferred_element_type=jnp.float32)  12.9 us
    all_to_all x1, blocking collectives, on_device(): lax.all_to_all(outgoing, 'expert', split_axis=0, concat_axis=0, tiled=True)  11.2 us
  transfers between devices with their start and end apart: 6, of which 6 were waited for; matrix products, arithmetic and copies ran while one was open for 2% of the time, Pallas kernels for 0%

profile of v1, /device:TPU:0, one launch (start us, length us, event | category | flops | bytes accessed | tf_op | source)
XLA Modules:
  0.0 379.5 jit_solution(8309466534994313140)
XLA Ops:
  7.2 0.8 select_reduce_fusion.1
  8.0 0.2 convert_reduce_fusion
  8.2 1.1 convolution_convert_fusion.2
  9.4 0.7 reshape.106
  10.1 7.3 %all-to-all-start = ((bf16[128,4,128]{2,1,0:T(4,128)(2,1)}), bf16[128,4,128]{2,1,0:T(4,128)(2,1)S(1)}, u32[]{:S(2)}, u32[]{:S(2)}) async-start(bf16[128,4,128]{2,1,0:T(4,128)(2,1)} %reshape.106), calls=%async_computation | async-start | bytes 262144 | tf_op jit(solution)/shard_map/all_to_all | solution.py:92
  17.3 0.9 reshape.105
  18.2 0.7 iota_compare_fusion.4
  18.9 2.0 fusion.61
  20.9 0.9 fusion.45
  22.0 0.1 copy.110
  22.1 2.6 all-to-all-done
  24.7 1.6 bitcast_reduce_fusion
  26.3 0.5 fusion.17
  26.8 0.7 reshape.116
  27.5 3.4 all-to-all-start.1
  31.0 1.6 fusion.18
  32.6 0.9 copy.121
  33.5 4.1 %all-to-all-done.1 = f32[8,16,4]{1,2,0:T(4,128)S(1)} async-done(((f32[8,16,4]{1,2,0:T(4,128)}), f32[8,16,4]{1,2,0:T(4,128)S(1)}, u32[]{:S(2)}, u32[]{:S(2)}) %all-to-all-start.1) | async-done | bytes 2080 | tf_op jit(solution)/shard_map/all_to_all | solution.py:98
  37.5 3.4 all-to-all-start.2
  41.0 0.2 fusion.35
  41.3 0.1 copy.111
  41.5 0.2 subtract_exponential_fusion.1
  41.8 0.1 copy.113
  41.9 0.1 copy.123
  42.0 0.1 copy.119
  42.1 7.0 %all-to-all-done.2 = f32[128,4,128]{2,1,0:T(4,128)S(1)} async-done(((f32[128,4,128]{2,1,0:T(4,128)}), f32[128,4,128]{2,1,0:T(4,128)S(1)}, u32[]{:S(2)}, u32[]{:S(2)}) %all-to-all-start.2) | async-done | bytes 262176 | tf_op jit(solution)/shard_map/all_to_all | solution.py:97
  49.1 0.2 fusion.30
  49.4 0.5 fusion.23
  49.9 31.7 %all_gather.3 = bf16[512,512]{1,0:T(8,128)(2,1)S(1)} all-gather(bf16[64,512]{1,0:T(8,128)(2,1)S(1)} %bitcast.105), channel_id=1, replica_groups=mesh['cache'=8,'expert'=4] {'cache'}, dimensions={0}, use_global_device_ids=true | all-gather | bytes 589824 | tf_op jit(solution)/shard_map/all_gather | solution.py:111
  81.6 0.4 convolution_convert_fusion.1
  82.0 13.0 %all_to_all.64 = bf16[8,64,512]{2,1,0:T(8,128)(2,1)S(1)} all-to-all(bf16[8,64,512]{2,1,0:T(8,128)(2,1)S(1)} %bitcast.95), channel_id=1, replica_groups=mesh['cache'=8,'expert'=4] {'cache'}, dimensions={0} | all-to-all | bytes 1048576 | tf_op jit(solution)/shard_map/all_to_all | solution.py:115
  95.1 0.8 copy.136
  96.1 0.1 eq.80
  96.2 0.2 convert_reduce_fusion.1
  96.4 0.1 copy.127
  96.6 20.2 %reduce-scatter.3.cloned.1.call-done = bf16[16,4096]{1,0:T(8,128)(2,1)} async-done(((bf16[64,4096]{1,0:T(8,128)(2,1)}), bf16[16,4096]{1,0:T(8,128)(2,1)}) %reduce-scatter.3.cloned.1.call-update) | async-done | bytes 131088 | tf_op jit(solution)/shard_map/reduce_scatter | solution.py:118
  116.8 1.1 multiply_reduce_fusion
  117.9 1.2 convolution_convert_fusion
  119.1 11.2 %all_to_all.65 = bf16[4,16,4096]{2,1,0:T(8,128)(2,1)S(1)} all-to-all(bf16[4,16,4096]{2,1,0:T(8,128)(2,1)S(1)} %bitcast.99), channel_id=1, replica_groups=mesh['cache'=8,'expert'=4] {'expert'}, dimensions={0} | all-to-all | bytes 1048576 | tf_op jit(solution)/shard_map/all_to_all | solution.py:135
  130.4 0.5 stack.5
  130.9 98.4 %all_to_all.66 = bf16[8,64,4096]{2,1,0:T(8,128)(2,1)S(1)} all-to-all(bf16[8,64,4096]{2,1,0:T(8,128)(2,1)S(1)} %stack.5), channel_id=1, replica_groups=mesh['cache'=8,'expert'=4] {'cache'}, dimensions={0} | all-to-all | bytes 8388608 | tf_op jit(solution)/shard_map/all_to_all | solution.py:138
  229.3 2.0 copy-done.2
  231.2 12.9 %fusion.4 = f32[512,1792]{1,0:T(8,128)} fusion(bf16[512,4096]{1,0:T(8,128)(2,1)S(1)} %bitcast.93, bf16[1,4096,1792]{2,1,0:T(8,128)(2,1)} %param.33), kind=kOutput, calls=%fused_computation.4 | convolution fusion | flops 7516192768 | bytes 22544384 | tf_op jit(solution)/shard_map/dot_general | solution.py:140
  244.1 28.6 %fusion.6 = bf16[512,4096]{1,0:T(8,128)(2,1)} fusion(bf16[1,1792,4096]{2,1,0:T(8,128)(2,1)} %param.35, f32[512,1792]{1,0:T(8,128)} %fusion.4, bf16[512,4096]{1,0:T(8,128)(2,1)} %bitcast.94, bf16[1,4096,1792]{2,1,0:T(8,128)(2,1)} %param.34), kind=kOutput, calls=%fused_computation.6 | convolution fusion | flops 15039987712 | bytes 41418752 | tf_op jit(solution)/shard_map/dot_general | solution.py:143
  272.8 86.6 %reduce-scatter.5.cloned.1.call-done = bf16[64,4096]{1,0:T(8,128)(2,1)} async-done(((bf16[512,4096]{1,0:T(8,128)(2,1)}), bf16[64,4096]{1,0:T(8,128)(2,1)}) %reduce-scatter.5.cloned.1.call-update) | async-done | bytes 524304 | tf_op jit(solution)/shard_map/reduce_scatter | solution.py:144
  359.4 3.5 all-to-all-start.6
  363.0 8.7 %all-to-all-done.6 = bf16[4,16,4096]{2,1,0:T(8,128)(2,1)S(1)} async-done(((bf16[4,16,4096]{2,1,0:T(8,128)(2,1)}), bf16[4,16,4096]{2,1,0:T(8,128)(2,1)S(1)}, u32[]{:S(2)}, u32[]{:S(2)}) %all-to-all-start.6) | async-done | bytes 524320 | tf_op jit(solution)/shard_map/all_to_all | solution.py:147
  371.7 1.0 fusion.9
  (44 shorter events, 0.9 us)
Async XLA Ops:
  7.2 42.2 %copy-start = (bf16[64,64,128]{2,1,0:T(8,128)(2,1)S(1)}, bf16[64,64,128]{2,1,0:T(8,128)(2,1)}, u32[]{:S(2)}) copy-start(bf16[64,64,128]{2,1,0:T(8,128)(2,1)} %param.22) | copy-start | bytes 3145732
  10.1 14.6 %all-to-all-start = ((bf16[128,4,128]{2,1,0:T(4,128)(2,1)}), bf16[128,4,128]{2,1,0:T(4,128)(2,1)S(1)}, u32[]{:S(2)}, u32[]{:S(2)}) async-start(bf16[128,4,128]{2,1,0:T(4,128)(2,1)} %reshape.106), calls=%async_computation | async-start | bytes 262144 | tf_op jit(solution)/shard_map/all_to_all | solution.py:92
  26.3 15.2 %copy-start.7 = (bf16[64,128]{1,0:T(8,128)(2,1)S(1)}, bf16[64,128]{1,0:T(8,128)(2,1)}, u32[]{:S(2)}) copy-start(bf16[64,128]{1,0:T(8,128)(2,1)} %param.20) | copy-start | bytes 49156
  27.5 10.0 %all-to-all-start.1 = ((f32[8,16,4]{1,2,0:T(4,128)}), f32[8,16,4]{1,2,0:T(4,128)S(1)}, u32[]{:S(2)}, u32[]{:S(2)}) async-start(f32[8,16,4]{1,2,0:T(4,128)} %reshape.116), calls=%async_computation.1 | async-start | bytes 32768 | tf_op jit(solution)/shard_map/all_to_all | solution.py:98
  32.5 49.0 %copy-start.5 = (bf16[512,512]{1,0:T(8,128)(2,1)S(1)}, bf16[512,512]{1,0:T(8,128)(2,1)}, u32[]{:S(2)}) copy-start(bf16[512,512]{1,0:T(8,128)(2,1)} %param.28) | copy-start | bytes 1572868
  37.5 11.6 %all-to-all-start.2 = ((f32[128,4,128]{2,1,0:T(4,128)}), f32[128,4,128]{2,1,0:T(4,128)S(1)}, u32[]{:S(2)}, u32[]{:S(2)}) async-start(f32[128,4,128]{2,1,0:T(4,128)} %copy.121), calls=%async_computation.2 | async-start | bytes 524288 | tf_op jit(solution)/shard_map/all_to_all | solution.py:97
  41.0 75.8 %reduce-scatter.3.cloned.1.call-start = ((), (), s32[]{:S(2)}) async-start(), calls=%async_computation.9 | async-start | bytes 655360 | tf_op jit(solution)/shard_map/reduce_scatter | solution.py:118
  49.4 46.6 %copy-start.9 = (s32[16,2]{0,1:T(2,128)S(1)}, s32[16,2]{0,1:T(2,128)}, u32[]{:S(2)}) copy-start(s32[16,2]{0,1:T(2,128)} %param.31) | copy-start | bytes 388
  49.4 67.4 %copy-start.3 = (bf16[16,4096]{1,0:T(8,128)(2,1)S(1)}, bf16[16,4096]{1,0:T(8,128)(2,1)}, u32[]{:S(2)}) copy-start(bf16[16,4096]{1,0:T(8,128)(2,1)} %param.29) | copy-start | bytes 393220
  49.4 68.5 %copy-start.8 = (f32[4096]{0:T(1024)S(1)}, f32[4096]{0:T(1024)}, u32[]{:S(2)}) copy-start(f32[4096]{0:T(1024)} %param.30) | copy-start | bytes 49156
  49.9 81.0 %copy-start.6 = (bf16[8,8,4,128]{3,1,2,0:T(8,128)(2,1)}, bf16[8,8,4,128]{3,1,2,0:T(8,128)(2,1)S(1)}, u32[]{:S(2)}) copy-start(bf16[8,8,4,128]{3,1,2,0:T(8,128)(2,1)S(1)} %copy.150) | copy-start | bytes 196612
  95.9 263.5 %reduce-scatter.5.cloned.1.call-start = ((), (), s32[]{:S(2)}) async-start(), calls=%async_computation.10 | async-start | bytes 4718592 | tf_op jit(solution)/shard_map/reduce_scatter | solution.py:144
  229.2 2.0 copy-start.2
  244.1 128.5 %copy-start.1 = (bf16[64,64,128]{2,1,0:T(8,128)(2,1)S(1)}, bf16[64,64,128]{2,1,0:T(8,128)(2,1)}, u32[]{:S(2)}) copy-start(bf16[64,64,128]{2,1,0:T(8,128)(2,1)} %param.22) | copy-start | bytes 3145732
  272.8 90.1 %copy-start.10 = (f32[16,2]{0,1:T(2,128)S(1)}, f32[16,2]{0,1:T(2,128)}, u32[]{:S(2)}) copy-start(f32[16,2]{0,1:T(2,128)} %param.32) | copy-start | bytes 388
  272.8 98.9 %copy-start.4 = (bf16[16,4096]{1,0:T(8,128)(2,1)S(1)}, bf16[16,4096]{1,0:T(8,128)(2,1)}, u32[]{:S(2)}) copy-start(bf16[16,4096]{1,0:T(8,128)(2,1)} %reduce-scatter.3.cloned.1.call-done) | copy-start | bytes 393220
  359.4 12.3 %all-to-all-start.6 = ((bf16[4,16,4096]{2,1,0:T(8,128)(2,1)}), bf16[4,16,4096]{2,1,0:T(8,128)(2,1)S(1)}, u32[]{:S(2)}, u32[]{:S(2)}) async-start(bf16[4,16,4096]{2,1,0:T(8,128)(2,1)} %bitcast.103), calls=%async_computation.8 | async-start | bytes 1048576 | tf_op jit(solution)/shard_map/all_to_all | solution.py:147
Sparse Core Ops, SparseCore 0:
  96.0 20.7 reduce-scatter.2
  272.9 86.4 reduce-scatter.4
